TPU v7x, 16 devices: a whole 2x2x2 slice. The times are simulated.
16 devices in a mesh: rep: 1, dp: 16 (over x, y, z, core).
Axes of the slice: x: 2, y: 2, z: 2, core: 2. Of those that a mesh axis runs over, the one named last changes fastest.
Arguments:
- x: bfloat16 [16, 2048, 1024], P(('rep', 'dp'))
- dy: bfloat16 [16, 2048, 1024], P(('rep', 'dp'))
- w_gate: bfloat16 [2, 1024, 2560], P(None, 'dp')
- w_up: bfloat16 [2, 1024, 2560], P(None, 'dp')
- w_down: bfloat16 [2, 2560, 1024], P(None, 'dp')
Outputs:
- output 1: bfloat16 [16, 2048, 1024], P(('rep', 'dp'))
- output 2: bfloat16 [2, 1024, 2560], P('rep', 'dp')
- output 3: bfloat16 [2, 1024, 2560], P('rep', 'dp')
- output 4: bfloat16 [2, 2560, 1024], P('rep', 'dp')
All inputs are finite; a program needn't handle non-finite values.
Results may differ from a plain program's by a relative error of at most 0.018.
Values are sent between devices in bfloat16 or wider.
A program may use at most 2 GiB of HBM per device.

v0:
```python
import jax
import jax.numpy as jnp
from jax import lax

NAMES = ("w_gate", "w_up", "w_down")


def matmul(a, w):
    return jnp.dot(a, w, preferred_element_type=jnp.float32).astype(jnp.bfloat16)


def normed(h):
    wide = h.astype(jnp.float32)
    scale = lax.rsqrt(jnp.mean(wide**2, -1, keepdims=True) + 1e-6)
    return (wide * scale).astype(jnp.bfloat16)


def layer(h, w):
    a = normed(h)
    gate = jnp.dot(a, w["w_gate"], preferred_element_type=jnp.float32)
    up = jnp.dot(a, w["w_up"], preferred_element_type=jnp.float32)
    return h + matmul((jax.nn.silu(gate) * up).astype(jnp.bfloat16), w["w_down"])


def stack(weights, h):
    for number in range(weights["w_gate"].shape[0]):
        h = layer(h, {name: w[number] for name, w in weights.items()})
    return h


def solution(mesh):
    groups = mesh.shape["rep"]

    def step(x, dy, *weights):
        shape = x.shape
        x, dy = (t.reshape(groups, -1, *t.shape[1:]) for t in (x, dy))

        def of_a_group(x, dy):
            _, back = jax.vjp(stack, dict(zip(NAMES, weights, strict=True)), x)
            by_weights, by_x = back(dy)
            return (by_x, *(by_weights[name] for name in NAMES))

        by_x, *by_weights = jax.vmap(of_a_group)(x, dy)
        return (by_x.reshape(shape), *(t.reshape(-1, *t.shape[2:]) for t in by_weights))

    return step
```

profile of v0, /device:TPU:0, one launch (start us, length us, event | category | flops | bytes accessed | tf_op | source)
XLA Modules:
  0.0 1386.2 jit_solution(10373147206103609939)
XLA Ops:
  40.5 120.4 %while.13 = (bf16[1,2048,1024]{2,1,0:T(8,128)(2,1)}, bf16[1,160,1024]{2,1,0:T(8,128)(2,1)S(1)}, bf16[1,2048,2560]{1,2,0:T(8,128)(2,1)}, bf16[1,160,1024]{2,1,0:T...) while((bf16[1,2048,1024]{2,1,0:T(8,128)(2,1)}, ...), condition=%wide.windowed_dot_general_cond_ag, body=%wide.windowed_dot_general_body_ag.sunk | while | flops 2685009920 | bytes 22807068 | solution.py:9
  94.6 12.8 collective-permute-start.2
  151.1 9.8 collective-permute-done.3
  160.9 13.7 copy.2
  174.6 19.0 %fusion.204 = f32[2048,2560]{1,0:T(8,128)} fusion(bf16[1,1024,2560]{2,1,0:T(8,128)(2,1)} %all-gather.27.cloned.1.call-done, bf16[1,2048,1024]{1,2,0:T(8,128)(2,1)} %fusion.187), kind=kOutput, calls=%fused_computation.257 | convolution fusion | flops 10737418240 | bytes 30408704 | tf_op jit(solution)/vmap(jvp())/dot_general | solution.py:20
  193.6 28.3 %fusion.176 = (bf16[1,2048,2560]{2,1,0:T(8,128)(2,1)}, f32[2048,2560]{1,0:T(8,128)}) fusion(f32[2048,2560]{1,0:T(8,128)} %fusion.204, bf16[1,1024,2560]{2,1,0:T(8,128)(2,1)} %all-gather.29.cloned.1.call-done, bf16[1,2048,1024]{1,2,0:T(8,128)(2,1)} %fusion.187), kind=kOutput, calls=%fused_computation.215 | convolution fusion | flops 10768875520 | bytes 61865984 | tf_op jit(solution)/vmap(jvp())/dot_general | solution.py:21
  221.9 14.5 %copy.6 = bf16[1,2048,2560]{1,2,0:T(8,128)(2,1)} copy(bf16[1,2048,2560]{2,1,0:T(8,128)(2,1)} %get-tuple-element.281) | data formatting | bytes 20971520
  236.4 16.7 %fusion.189 = (f32[2048]{0:T(1024)S(1)}, bf16[1,2048,1024]{1,2,0:T(8,128)(2,1)S(1)}) fusion(bf16[1,2048,1024]{1,2,0:T(8,128)(2,1)} %copy.1, bf16[1,2560,1024]{2,1,0:T(8,128)(2,1)} %all-gather.31.cloned.1.call-done, bf16[1,2048,2560]{2,1,0:T(8,128)(2,1)} %get-tuple-element.281), kind=kOutput, calls=%fused_computation.242 | convolution fusion | flops 10747901952 | bytes 24125440 | tf_op jit(solution)/vmap(jvp())/dot_general | solution.py:9
  258.3 18.7 %fusion.196 = f32[2048,2560]{1,0:T(8,128)} fusion(bf16[1,1024,2560]{2,1,0:T(8,128)(2,1)} %all-gather.33.cloned.1.call-done, bf16[1,2048,1024]{1,2,0:T(8,128)(2,1)} %fusion.190), kind=kOutput, calls=%fused_computation.249 | convolution fusion | flops 10737418240 | bytes 30408704 | tf_op jit(solution)/vmap(jvp())/dot_general | solution.py:20
  277.0 28.3 %fusion.170 = (bf16[1,2048,2560]{2,1,0:T(8,128)(2,1)}, f32[2048,2560]{1,0:T(8,128)}) fusion(f32[2048,2560]{1,0:T(8,128)} %fusion.196, bf16[1,1024,2560]{2,1,0:T(8,128)(2,1)} %all-gather.35.cloned.1.call-done, bf16[1,2048,1024]{1,2,0:T(8,128)(2,1)} %fusion.190), kind=kOutput, calls=%fused_computation.205 | convolution fusion | flops 10768875520 | bytes 61865984 | tf_op jit(solution)/vmap(jvp())/dot_general | solution.py:21
  305.4 14.6 %copy.4 = bf16[1,2048,2560]{1,2,0:T(8,128)(2,1)} copy(bf16[1,2048,2560]{2,1,0:T(8,128)(2,1)} %get-tuple-element.289) | data formatting | bytes 20971520
  320.0 138.2 %while.18 = (bf16[1,2048,2560]{1,2,0:T(8,128)(2,1)}, bf16[1,2048,1024]{2,1,0:T(8,128)(2,1)}, f32[160,1024]{1,0:T(8,128)S(1)}, f32[160,1024]{1,0:T(8,128)}, u32[]...) while((bf16[1,2048,2560]{1,2,0:T(8,128)(2,1)}, ...), condition=%wide.windowed_dot_general_cond_rs.4.clone, body=%wide.windowed_dot_general_body_rs.4.clone.sunk | while | flops 2690580480 | bytes 52953680 | solution.py:9
  334.1 12.5 collective-permute-start.22
  390.4 9.0 collective-permute-start.20
  425.5 9.0 collective-permute-start.20
  458.2 8.9 collective-permute-start.33
  467.2 19.0 %convert_multiply_fusion.3 = (bf16[1,2048,2560]{2,1,0:T(8,128)(2,1)S(1)}, bf16[1,2048,2560]{2,1,0:T(8,128)(2,1)S(1)}) fusion(f32[2048,2560]{1,0:T(8,128)} %fusion.196, bf16[1,2048,2560]{2,1,0:T(8,128)(2,1)} %copy.2, f32[2048,2560]{1,0:T(8,128)} %get-tuple-element.290), kind=kLoop, calls=%fused_computation.193 | loop fusion | flops 78643200 | bytes 73400320 | tf_op jit(solution)/vmap(transpose(jvp()))/mul | solution.py:22
  486.2 15.6 %fusion.168 = bf16[2048,1024]{0,1:T(8,128)(2,1)} fusion(bf16[1,2048,2560]{2,1,0:T(8,128)(2,1)S(1)} %get-tuple-element.622, bf16[1,1024,2560]{2,1,0:T(8,128)(2,1)} %all-gather.33.cloned.1.call-done), kind=kOutput, calls=%fused_computation.202 | convolution fusion | flops 10737418240 | bytes 19922944 | tf_op jit(solution)/vmap(transpose(jvp()))/dot_general | solution.py:20
  501.9 16.2 %fusion.191 = (f32[2048]{0:T(1024)S(1)}, bf16[2048,1024]{0,1:T(8,128)(2,1)}) fusion(bf16[1,2048,1024]{1,2,0:T(8,128)(2,1)} %copy-done.25, bf16[2048,1024]{0,1:T(8,128)(2,1)} %fusion.168, bf16[1,1024,2560]{2,1,0:T(8,128)(2,1)} %all-gather.35.cloned.1.call-done, bf16[1,2048,2560]{2,1,0:T(8,128)(2,1)S(1)} %get-tuple-element.694), kind=kOutput, calls=%fused_computation.244 | convolution fusion | flops 10747901952 | bytes 28319744 | tf_op jit(solution)/vmap(transpose(jvp()))/dot_general | solution.py:21
  530.9 140.2 %while.19 = (bf16[1,2048,1024]{2,1,0:T(8,128)(2,1)}, bf16[1,2048,2560]{1,2,0:T(8,128)(2,1)}, f32[1024,160]{0,1:T(8,128)S(1)}, f32[1024,160]{0,1:T(8,128)}, u32[]...) while((bf16[1,2048,1024]{2,1,0:T(8,128)(2,1)}, ...), condition=%wide.windowed_dot_general_cond_rs.5.clone, body=%wide.windowed_dot_general_body_rs.5.clone.sunk | while | flops 2690580480 | bytes 52953680 | solution.py:9
  544.1 13.9 %collective-permute-start.26 = (f32[1024,160]{0,1:T(8,128)S(1)}, f32[1024,160]{0,1:T(8,128)S(1)}, u32[]{:S(2)}, u32[]{:S(2)}) collective-permute-start(f32[1024,160]{0,1:T(8,128)S(1)} %get-tuple-element.552), channel_id=51, source_target_pairs={{0,1},{1,2},{2,3},{3,4},{4,5},{5,6},{6,7},{7,8},{8,9},{9,10},{10,1... | collective-permute-start | bytes 1966088 | tf_op jit(solution)/vmap(transpose(jvp()))/dot_general | solution.py:9
  601.1 8.9 collective-permute-start.24
  636.9 8.9 collective-permute-start.24
  679.9 143.6 %while.16 = (bf16[1,2048,2560]{2,1,0:T(8,128)(2,1)}, bf16[1,2048,1024]{1,2,0:T(8,128)(2,1)}, f32[2560,64]{0,1:T(8,128)S(1)}, f32[2560,64]{0,1:T(8,128)}, u32[]{:...) while((bf16[1,2048,2560]{2,1,0:T(8,128)(2,1)}, ...), condition=%wide.windowed_dot_general_cond_rs.2.clone, body=%wide.windowed_dot_general_body_rs.2.clone.sunk | while | flops 2687434752 | bytes 101188280 | solution.py:21
  693.8 11.5 collective-permute-start.14
  831.4 32.1 %convert_multiply_fusion.1 = (bf16[1,2048,2560]{2,1,0:T(8,128)(2,1)}, bf16[1,2048,2560]{2,1,0:T(8,128)(2,1)}) fusion(f32[2048,2560]{1,0:T(8,128)} %fusion.204, f32[2048,2560]{1,0:T(8,128)} %get-tuple-element.282, bf16[1,2560,1024]{2,1,0:T(8,128)(2,1)} %all-gather.31.cloned.1.call-done, bf16[1,2048,1024]{1,2,0:T(8,128)(2,1)} %fusion.207), kind=kOutput, calls=%fused_computation.191 | convolution fusion | flops 10821304320 | bytes 72351744 | tf_op jit(solution)/vmap(transpose(jvp()))/dot_general | solution.py:9
  863.5 144.1 %while.17 = (bf16[1,2048,2560]{2,1,0:T(8,128)(2,1)}, bf16[1,2048,1024]{1,2,0:T(8,128)(2,1)}, f32[2560,64]{0,1:T(8,128)S(1)}, f32[2560,64]{0,1:T(8,128)}, u32[]{:...) while((bf16[1,2048,2560]{2,1,0:T(8,128)(2,1)}, ...), condition=%wide.windowed_dot_general_cond_rs.3.clone, body=%wide.windowed_dot_general_body_rs.3.clone.sunk | while | flops 2687434752 | bytes 101188280 | solution.py:21
  878.2 10.1 collective-permute-start.18
  1008.5 147.5 %while.14 = (bf16[1,2048,2560]{2,1,0:T(8,128)(2,1)}, bf16[1,2048,1024]{1,2,0:T(8,128)(2,1)}, f32[2560,64]{0,1:T(8,128)S(1)}, f32[2560,64]{0,1:T(8,128)}, u32[]{:...) while((bf16[1,2048,2560]{2,1,0:T(8,128)(2,1)}, ...), condition=%wide.windowed_dot_general_cond_rs.clone, body=%wide.windowed_dot_general_body_rs.clone.sunk | while | flops 2687434752 | bytes 101188280 | solution.py:20
  1156.9 149.1 %while.15 = (bf16[1,2048,2560]{2,1,0:T(8,128)(2,1)}, bf16[1,2048,1024]{1,2,0:T(8,128)(2,1)}, f32[2560,64]{0,1:T(8,128)}, f32[2560,64]{0,1:T(8,128)}, u32[]{:T(12...) while((bf16[1,2048,2560]{2,1,0:T(8,128)(2,1)}, ...), condition=%wide.windowed_dot_general_cond_rs.1.clone, body=%wide.windowed_dot_general_body_rs.1.clone.sunk | while | flops 2687434752 | bytes 101188280 | solution.py:20
  1314.1 16.6 %fusion.164 = bf16[2048,1024]{0,1:T(8,128)(2,1)} fusion(bf16[1,2048,2560]{2,1,0:T(8,128)(2,1)} %get-tuple-element.810, bf16[1,1024,2560]{2,1,0:T(8,128)(2,1)} %all-gather.27.cloned.1.call-done), kind=kOutput, calls=%fused_computation.198 | convolution fusion | flops 10737418240 | bytes 19922944 | tf_op jit(solution)/vmap(transpose(jvp()))/dot_general | solution.py:20
  1330.8 15.8 %fusion.188 = (f32[2048]{0:T(1024)S(1)}, bf16[2048,1024]{0,1:T(8,128)(2,1)}) fusion(bf16[1,2048,1024]{1,2,0:T(8,128)(2,1)S(1)} %copy-done.7, bf16[2048,1024]{0,1:T(8,128)(2,1)} %fusion.164, bf16[1,1024,2560]{2,1,0:T(8,128)(2,1)} %all-gather.29.cloned.1.call-done, bf16[1,2048,2560]{2,1,0:T(8,128)(2,1)S(1)} %bitcast.592), kind=kOutput, calls=%fused_computation.241 | convolution fusion | flops 10747901952 | bytes 28319744 | tf_op jit(solution)/vmap(transpose(jvp()))/dot_general | solution.py:21
  (667 shorter events, 984.7 us)
Async XLA Ops:
  7.2 167.4 %all-gather.27.cloned.1.call-start = ((), (), s32[]{:S(2)}) async-start(), calls=%async_computation | async-start | bytes 5570560 | tf_op jit(solution)/vmap(jvp())/squeeze | solution.py:27
  9.2 184.4 %all-gather.29.cloned.1.call-start = ((), (), s32[]{:S(2)}) async-start(), calls=%async_computation.1 | async-start | bytes 5570560 | tf_op jit(solution)/vmap(jvp())/squeeze | solution.py:27
  11.3 225.1 %all-gather.31.cloned.1.call-start = ((), (), s32[]{:S(2)}) async-start(), calls=%async_computation.2 | async-start | bytes 5570560 | tf_op jit(solution)/vmap(jvp())/squeeze | solution.py:27
  13.2 245.1 %all-gather.33.cloned.1.call-start = ((), (), s32[]{:S(2)}) async-start(), calls=%async_computation.3 | async-start | bytes 5570560 | tf_op jit(solution)/vmap(jvp())/squeeze | solution.py:27
  13.8 263.3 %all-gather.35.cloned.1.call-start = ((), (), s32[]{:S(2)}) async-start(), calls=%async_computation.4 | async-start | bytes 5570560 | tf_op jit(solution)/vmap(jvp())/squeeze | solution.py:27
  13.8 21.5 %collective-permute-start.28 = (bf16[1,160,1024]{2,1,0:T(8,128)(2,1)S(1)}, bf16[1,160,1024]{2,1,0:T(8,128)(2,1)S(1)}, u32[]{:S(2)}, u32[]{:S(2)}) collective-permute-start(bf16[1,160,1024]{2,1,0:T(8,128)(2,1)S(1)} %get-tuple-element.557), channel_id=6, source_target_pairs={{0,1},{1,2},{2,3},{3,4},{4,5},{5,6},{6,7},{7,8},{8,9},{9,10},{10,1... | collective-permute-start | bytes 983048 | tf_op jit(solution)/vmap(transpose(jvp()))/dot_general | solution.py:9
  94.6 18.4 %collective-permute-start = (bf16[1,160,1024]{2,1,0:T(8,128)(2,1)S(1)}, bf16[1,160,1024]{2,1,0:T(8,128)(2,1)S(1)}, u32[]{:S(2)}, u32[]{:S(2)}) collective-permute-start(bf16[1,160,1024]{2,1,0:T(8,128)(2,1)S(1)} %get-tuple-element.567), channel_id=7, source_target_pairs={{0,15},{1,0},{2,1},{3,2},{4,3},{5,4},{6,5},{7,6},{8,7},{9,8},{10,9... | collective-permute-start | bytes 983048 | tf_op jit(solution)/vmap(transpose(jvp()))/dot_general | solution.py:9
  94.6 18.4 %collective-permute-start.2 = (bf16[1,160,1024]{2,1,0:T(8,128)(2,1)S(1)}, bf16[1,160,1024]{2,1,0:T(8,128)(2,1)S(1)}, u32[]{:S(2)}, u32[]{:S(2)}) collective-permute-start(bf16[1,160,1024]{2,1,0:T(8,128)(2,1)S(1)} %get-tuple-element.569), channel_id=8, source_target_pairs={{0,1},{1,2},{2,3},{3,4},{4,5},{5,6},{6,7},{7,8},{8,9},{9,10},{10,1... | collective-permute-start | bytes 983048 | tf_op jit(solution)/vmap(transpose(jvp()))/dot_general | solution.py:9
  144.1 16.8 %collective-permute-start.3 = (bf16[1,160,1024]{2,1,0:T(8,128)(2,1)S(1)}, bf16[1,160,1024]{2,1,0:T(8,128)(2,1)S(1)}, u32[]{:S(2)}, u32[]{:S(2)}) collective-permute-start(bf16[1,160,1024]{2,1,0:T(8,128)(2,1)S(1)} %collective-permute-done.2), channel_id=10, source_target_pairs={{0,1},{1,2},{2,3},{3,4},{4,5},{5,6},{6,7},{7,8},{8,9},{9,10},{10,1... | collective-permute-start | bytes 983048 | tf_op jit(solution)/vmap(transpose(jvp()))/dot_general | solution.py:9
  334.1 16.6 %collective-permute-start.22 = (f32[160,1024]{1,0:T(8,128)S(1)}, f32[160,1024]{1,0:T(8,128)S(1)}, u32[]{:S(2)}, u32[]{:S(2)}) collective-permute-start(f32[160,1024]{1,0:T(8,128)S(1)} %get-tuple-element.543), channel_id=45, source_target_pairs={{0,1},{1,2},{2,3},{3,4},{4,5},{5,6},{6,7},{7,8},{8,9},{9,10},{10,1... | collective-permute-start | bytes 1966088 | tf_op jit(solution)/vmap(transpose(jvp()))/dot_general | solution.py:9
  390.4 13.2 collective-permute-start.20
  425.5 13.2 collective-permute-start.20
  458.2 904.4 %collective-permute-start.33 = (f32[160,1024]{1,0:T(8,128)}, f32[160,1024]{1,0:T(8,128)}, u32[]{:S(2)}, u32[]{:S(2)}) collective-permute-start(f32[160,1024]{1,0:T(8,128)} %get-tuple-element.52), channel_id=46, source_target_pairs={{0,1},{1,2},{2,3},{3,4},{4,5},{5,6},{6,7},{7,8},{8,9},{9,10},{10,1... | collective-permute-start | bytes 1966088 | tf_op jit(solution)/vmap(transpose(jvp()))/dot_general | solution.py:9
  544.1 18.0 %collective-permute-start.26 = (f32[1024,160]{0,1:T(8,128)S(1)}, f32[1024,160]{0,1:T(8,128)S(1)}, u32[]{:S(2)}, u32[]{:S(2)}) collective-permute-start(f32[1024,160]{0,1:T(8,128)S(1)} %get-tuple-element.552), channel_id=51, source_target_pairs={{0,1},{1,2},{2,3},{3,4},{4,5},{5,6},{6,7},{7,8},{8,9},{9,10},{10,1... | collective-permute-start | bytes 1966088 | tf_op jit(solution)/vmap(transpose(jvp()))/dot_general | solution.py:9
  671.1 695.2 %collective-permute-start.34 = (f32[1024,160]{0,1:T(8,128)}, f32[1024,160]{0,1:T(8,128)}, u32[]{:S(2)}, u32[]{:S(2)}) collective-permute-start(f32[1024,160]{0,1:T(8,128)} %get-tuple-element.54), channel_id=52, source_target_pairs={{0,1},{1,2},{2,3},{3,4},{4,5},{5,6},{6,7},{7,8},{8,9},{9,10},{10,1... | collective-permute-start | bytes 1966088 | tf_op jit(solution)/vmap(transpose(jvp()))/dot_general | solution.py:9
  693.8 13.2 collective-permute-start.14
  715.6 14.7 %collective-permute-start.12 = (f32[2560,64]{0,1:T(8,128)S(1)}, f32[2560,64]{0,1:T(8,128)}, u32[]{:S(2)}, u32[]{:S(2)}) collective-permute-start(f32[2560,64]{0,1:T(8,128)S(1)} %broadcast_select_fusion.28), channel_id=31, source_target_pairs={{0,1},{1,2},{2,3},{3,4},{4,5},{5,6},{6,7},{7,8},{8,9},{9,10},{10,1... | collective-permute-start | bytes 1966088 | tf_op jit(solution)/vmap(transpose(jvp()))/dot_general | solution.py:21
  752.2 14.7 %collective-permute-start.12 = (f32[2560,64]{0,1:T(8,128)S(1)}, f32[2560,64]{0,1:T(8,128)}, u32[]{:S(2)}, u32[]{:S(2)}) collective-permute-start(f32[2560,64]{0,1:T(8,128)S(1)} %broadcast_select_fusion.28), channel_id=31, source_target_pairs={{0,1},{1,2},{2,3},{3,4},{4,5},{5,6},{6,7},{7,8},{8,9},{9,10},{10,1... | collective-permute-start | bytes 1966088 | tf_op jit(solution)/vmap(transpose(jvp()))/dot_general | solution.py:21
  788.3 14.7 %collective-permute-start.12 = (f32[2560,64]{0,1:T(8,128)S(1)}, f32[2560,64]{0,1:T(8,128)}, u32[]{:S(2)}, u32[]{:S(2)}) collective-permute-start(f32[2560,64]{0,1:T(8,128)S(1)} %broadcast_select_fusion.28), channel_id=31, source_target_pairs={{0,1},{1,2},{2,3},{3,4},{4,5},{5,6},{6,7},{7,8},{8,9},{9,10},{10,1... | collective-permute-start | bytes 1966088 | tf_op jit(solution)/vmap(transpose(jvp()))/dot_general | solution.py:21
  823.5 540.4 %collective-permute-start.31 = (f32[2560,64]{0,1:T(8,128)}, f32[2560,64]{0,1:T(8,128)}, u32[]{:S(2)}, u32[]{:S(2)}) collective-permute-start(f32[2560,64]{0,1:T(8,128)} %get-tuple-element.48), channel_id=34, source_target_pairs={{0,1},{1,2},{2,3},{3,4},{4,5},{5,6},{6,7},{7,8},{8,9},{9,10},{10,1... | collective-permute-start | bytes 1966088 | tf_op jit(solution)/vmap(transpose(jvp()))/dot_general | solution.py:21
  935.6 14.1 %collective-permute-start.16 = (f32[2560,64]{0,1:T(8,128)}, f32[2560,64]{0,1:T(8,128)}, u32[]{:S(2)}, u32[]{:S(2)}) collective-permute-start(f32[2560,64]{0,1:T(8,128)} %broadcast_select_fusion.30), channel_id=37, source_target_pairs={{0,1},{1,2},{2,3},{3,4},{4,5},{5,6},{6,7},{7,8},{8,9},{9,10},{10,1... | collective-permute-start | bytes 1966088 | tf_op jit(solution)/vmap(transpose(jvp()))/dot_general | solution.py:21
  972.5 14.5 %collective-permute-start.16 = (f32[2560,64]{0,1:T(8,128)}, f32[2560,64]{0,1:T(8,128)}, u32[]{:S(2)}, u32[]{:S(2)}) collective-permute-start(f32[2560,64]{0,1:T(8,128)} %broadcast_select_fusion.30), channel_id=37, source_target_pairs={{0,1},{1,2},{2,3},{3,4},{4,5},{5,6},{6,7},{7,8},{8,9},{9,10},{10,1... | collective-permute-start | bytes 1966088 | tf_op jit(solution)/vmap(transpose(jvp()))/dot_general | solution.py:21
  1009.7 14.1 %collective-permute-start.4 = (f32[2560,64]{0,1:T(8,128)}, f32[2560,64]{0,1:T(8,128)}, u32[]{:S(2)}, u32[]{:S(2)}) collective-permute-start(f32[2560,64]{0,1:T(8,128)} %broadcast_select_fusion.24), channel_id=19, source_target_pairs={{0,1},{1,2},{2,3},{3,4},{4,5},{5,6},{6,7},{7,8},{8,9},{9,10},{10,1... | collective-permute-start | bytes 1966088 | tf_op jit(solution)/vmap(transpose(jvp()))/dot_general | solution.py:20
  1046.6 14.5 %collective-permute-start.4 = (f32[2560,64]{0,1:T(8,128)}, f32[2560,64]{0,1:T(8,128)}, u32[]{:S(2)}, u32[]{:S(2)}) collective-permute-start(f32[2560,64]{0,1:T(8,128)} %broadcast_select_fusion.24), channel_id=19, source_target_pairs={{0,1},{1,2},{2,3},{3,4},{4,5},{5,6},{6,7},{7,8},{8,9},{9,10},{10,1... | collective-permute-start | bytes 1966088 | tf_op jit(solution)/vmap(transpose(jvp()))/dot_general | solution.py:20
  1083.9 14.1 %collective-permute-start.4 = (f32[2560,64]{0,1:T(8,128)}, f32[2560,64]{0,1:T(8,128)}, u32[]{:S(2)}, u32[]{:S(2)}) collective-permute-start(f32[2560,64]{0,1:T(8,128)} %broadcast_select_fusion.24), channel_id=19, source_target_pairs={{0,1},{1,2},{2,3},{3,4},{4,5},{5,6},{6,7},{7,8},{8,9},{9,10},{10,1... | collective-permute-start | bytes 1966088 | tf_op jit(solution)/vmap(transpose(jvp()))/dot_general | solution.py:20
  1120.8 14.5 %collective-permute-start.4 = (f32[2560,64]{0,1:T(8,128)}, f32[2560,64]{0,1:T(8,128)}, u32[]{:S(2)}, u32[]{:S(2)}) collective-permute-start(f32[2560,64]{0,1:T(8,128)} %broadcast_select_fusion.24), channel_id=19, source_target_pairs={{0,1},{1,2},{2,3},{3,4},{4,5},{5,6},{6,7},{7,8},{8,9},{9,10},{10,1... | collective-permute-start | bytes 1966088 | tf_op jit(solution)/vmap(transpose(jvp()))/dot_general | solution.py:20
  1157.8 14.1 %collective-permute-start.8 = (f32[2560,64]{0,1:T(8,128)}, f32[2560,64]{0,1:T(8,128)}, u32[]{:S(2)}, u32[]{:S(2)}) collective-permute-start(f32[2560,64]{0,1:T(8,128)} %broadcast_select_fusion.26), channel_id=25, source_target_pairs={{0,1},{1,2},{2,3},{3,4},{4,5},{5,6},{6,7},{7,8},{8,9},{9,10},{10,1... | collective-permute-start | bytes 1966088 | tf_op jit(solution)/vmap(transpose(jvp()))/dot_general | solution.py:20
  1195.1 15.6 %collective-permute-start.8 = (f32[2560,64]{0,1:T(8,128)}, f32[2560,64]{0,1:T(8,128)}, u32[]{:S(2)}, u32[]{:S(2)}) collective-permute-start(f32[2560,64]{0,1:T(8,128)} %broadcast_select_fusion.26), channel_id=25, source_target_pairs={{0,1},{1,2},{2,3},{3,4},{4,5},{5,6},{6,7},{7,8},{8,9},{9,10},{10,1... | collective-permute-start | bytes 1966088 | tf_op jit(solution)/vmap(transpose(jvp()))/dot_general | solution.py:20
  1232.8 15.9 %collective-permute-start.8 = (f32[2560,64]{0,1:T(8,128)}, f32[2560,64]{0,1:T(8,128)}, u32[]{:S(2)}, u32[]{:S(2)}) collective-permute-start(f32[2560,64]{0,1:T(8,128)} %broadcast_select_fusion.26), channel_id=25, source_target_pairs={{0,1},{1,2},{2,3},{3,4},{4,5},{5,6},{6,7},{7,8},{8,9},{9,10},{10,1... | collective-permute-start | bytes 1966088 | tf_op jit(solution)/vmap(transpose(jvp()))/dot_general | solution.py:20
  1270.8 15.2 %collective-permute-start.8 = (f32[2560,64]{0,1:T(8,128)}, f32[2560,64]{0,1:T(8,128)}, u32[]{:S(2)}, u32[]{:S(2)}) collective-permute-start(f32[2560,64]{0,1:T(8,128)} %broadcast_select_fusion.26), channel_id=25, source_target_pairs={{0,1},{1,2},{2,3},{3,4},{4,5},{5,6},{6,7},{7,8},{8,9},{9,10},{10,1... | collective-permute-start | bytes 1966088 | tf_op jit(solution)/vmap(transpose(jvp()))/dot_general | solution.py:20
  1306.0 59.1 %collective-permute-start.32 = (f32[2560,64]{0,1:T(8,128)}, f32[2560,64]{0,1:T(8,128)}, u32[]{:S(2)}, u32[]{:S(2)}) collective-permute-start(f32[2560,64]{0,1:T(8,128)} %get-tuple-element.50), channel_id=40, source_target_pairs={{0,1},{1,2},{2,3},{3,4},{4,5},{5,6},{6,7},{7,8},{8,9},{9,10},{10,1... | collective-permute-start | bytes 1966088 | tf_op jit(solution)/vmap(transpose(jvp()))/dot_general | solution.py:21
  1362.6 15.6 %collective-permute-start.30 = (f32[2560,64]{0,1:T(8,128)S(1)}, f32[2560,64]{0,1:T(8,128)S(1)}, u32[]{:S(2)}, u32[]{:S(2)}) collective-permute-start(f32[2560,64]{0,1:T(8,128)S(1)} %copy-done.28), channel_id=28, source_target_pairs={{0,1},{1,2},{2,3},{3,4},{4,5},{5,6},{6,7},{7,8},{8,9},{9,10},{10,1... | collective-permute-start | bytes 1966088 | tf_op jit(solution)/vmap(transpose(jvp()))/dot_general | solution.py:20
  (192 other events, 2910.9 us)
Sparse Core Ops, SparseCore 0:
  10.2 48.6 all-gather.26
  61.1 51.5 all-gather.28
  114.9 52.6 all-gather.30
  169.8 38.5 all-gather.32
  210.4 38.3 all-gather.34
where the time goes:
time: 1400 us; the launch traced here: 1390 us
  starting transfers between devices  449 us (32%)
  matrix products  421 us (30%)
  waiting for transfers between devices  248 us (18%)
  other arithmetic  152 us (11%)
  local copies, waits for them, and re-layouts  99.5 us (7%)
  between operations  14.6 us (1%)
    dot_general x51, starting transfers between devices, matmul(): jnp.dot(a, w, preferred_element_type=jnp.float32).astype(jnp.bfloat16)  185 us
    dot_general x20, matrix products, layer(): up = jnp.dot(a, w['w_up'], preferred_element_type=jnp.float32)  148 us
    dot_general x26, matrix products, matmul(): jnp.dot(a, w, preferred_element_type=jnp.float32).astype(jnp.bfloat16)  145 us
    dot_general x34, starting transfers between devices, layer(): up = jnp.dot(a, w['w_up'], preferred_element_type=jnp.float32)  138 us
    dot_general x20, matrix products, layer(): gate = jnp.dot(a, w['w_gate'], preferred_element_type=jnp.float32)  129 us
    dot_general x34, starting transfers between devices, layer(): gate = jnp.dot(a, w['w_gate'], preferred_element_type=jnp.float32)  125 us
    dot_general x51, waiting for transfers between devices, matmul(): jnp.dot(a, w, preferred_element_type=jnp.float32).astype(jnp.bfloat16)  98.6 us
    dot_general x34, waiting for transfers between devices, layer(): gate = jnp.dot(a, w['w_gate'], preferred_element_type=jnp.float32)  79 us
  transfers between devices with their start and end apart: 124, of which 87 were waited for; matrix products, arithmetic and copies ran while one was open for 44% of the time, Pallas kernels for 0%

commit v1 on v0

v1 whole, which is shorter than its diff:
```python
import jax
import jax.numpy as jnp
from jax import lax
from jax.sharding import PartitionSpec as P

F32, BF16 = jnp.float32, jnp.bfloat16


def dot(a, b, dims):
    return lax.dot_general(a, b, (dims, ((), ())), preferred_element_type=F32)


def scale_of(h):
    wide = h.astype(F32)
    return lax.rsqrt(jnp.mean(wide * wide, -1, keepdims=True) + 1e-6)


def normed(h, scale):
    return (h.astype(F32) * scale).astype(BF16)


def solution(mesh):
    def step(x, dy, w_gate, w_up, w_down):
        layers = w_gate.shape[0]
        gather = lambda w: lax.all_gather(w, "dp", axis=0, tiled=True)
        scatter = lambda g: lax.psum_scatter(g, "dp", scatter_dimension=0, tiled=True)
        full = [tuple(gather(w[n]) for w in (w_gate, w_up, w_down)) for n in range(layers)]

        h = x[0]
        saved = []
        for n in range(layers):
            wg, wu, wd = full[n]
            scale = scale_of(h)
            a = normed(h, scale)
            gate = dot(a, wg, ((1,), (0,)))
            up = dot(a, wu, ((1,), (0,)))
            hidden = (jax.nn.silu(gate) * up).astype(BF16)
            saved.append((h, scale, a, gate, up, hidden))
            if n + 1 < layers:
                h = h + dot(hidden, wd, ((1,), (0,))).astype(BF16)

        g = dy[0]
        outs = []
        for n in reversed(range(layers)):
            wg, wu, wd = full[n]
            h, scale, a, gate, up, hidden = saved[n]
            by_wd = dot(hidden, g, ((0,), (0,))).astype(BF16)
            by_hidden = dot(g, wd, ((1,), (1,))).astype(BF16).astype(F32)
            s = jax.nn.sigmoid(gate)
            by_up = (by_hidden * gate * s).astype(BF16)
            by_gate = (by_hidden * up * s * (1 + gate * (1 - s))).astype(BF16)
            by_wg = dot(a, by_gate, ((0,), (0,))).astype(BF16)
            by_wu = dot(a, by_up, ((0,), (0,))).astype(BF16)
            by_a = dot(by_gate, wg, ((1,), (1,))) + dot(by_up, wu, ((1,), (1,)))
            by_a = by_a.astype(BF16).astype(F32)
            wide = h.astype(F32)
            along = jnp.mean(by_a * wide, -1, keepdims=True)
            g = (g.astype(F32) + (scale * (by_a - wide * (scale * scale * along))).astype(BF16).astype(F32)).astype(BF16)
            outs.append((scatter(by_wg), scatter(by_wu), scatter(by_wd)))
        outs = outs[::-1]
        return (g[None], *(jnp.stack([o[i] for o in outs]) for i in range(3)))

    rows, cols = P(("rep", "dp")), P(None, "dp")
    out = P("rep", "dp")
    return jax.shard_map(
        step, mesh=mesh, in_specs=(rows, rows, cols, cols, cols), out_specs=(rows, out, out, out), check_vma=False
    )
```

time: 1400 us -> 725 us (0.52)
  starting transfers between devices: 449 us -> 0.49 us
  other arithmetic: 152 us -> 17 us
  matrix products: 421 us -> 338 us
  waiting for transfers between devices: 248 us -> 321 us
  local copies, waits for them, and re-layouts: 99.5 us -> 28.9 us
    dot_general x119 -> x0, starting transfers between devices: 448 us -> none  [the longest x51 185 us: matmul(): jnp.dot(a, w, preferred_element_type=jnp.float32).astype(jnp.bfloat16)]
    dot_general x119 -> x0, waiting for transfers between devices: 248 us -> none  [the longest x51 98.6 us: matmul(): jnp.dot(a, w, preferred_element_type=jnp.float32).astype(jnp.bfloat16)]
    reduce_scatter x0 -> x6, waiting for transfers between devices: none -> 189 us  [step(): lax.psum_scatter(g, 'dp', scatter_dimension=0, tiled=True)]
    all_gather x0 -> x6, waiting for transfers between devices: none -> 130 us  [step(): gather = lambda w: lax.all_gather(w, 'dp', axis=0, tiled=True)]
    dot_general x112 -> x0, other arithmetic: 103 us -> none
    dot_general x66 -> x17, matrix products: 421 us -> 338 us  [dot(): return lax.dot_general(a, b, (dims, ((), ())), preferred_element_type=F32)]
    unnamed x78 -> x27, local copies, waits for them, and re-layouts: 60 us -> 23 us
    dot_general x146 -> x0, local copies, waits for them, and re-layouts: 33.7 us -> none  [the longest x18 33.5 us: matmul(): jnp.dot(a, w, preferred_element_type=jnp.float32).astype(jnp.bfloat16)]
  transfers between devices with their start and end apart: 124 -> 12, of which waited for: 87 -> 9; matrix products, arithmetic and copies ran while one was open for 44% -> 44% of each run, Pallas kernels for 0% -> 0%
where the time goes in v1:
time: 725 us; the launch traced here: 720 us
  matrix products  338 us (47%)
  waiting for transfers between devices  321 us (44%)
  local copies, waits for them, and re-layouts  28.9 us (4%)
  other arithmetic  17 us (2%)
  between operations  14.8 us (2%)
    dot_general x17, matrix products, dot(): return lax.dot_general(a, b, (dims, ((), ())), preferred_element_type=F32)  338 us
    reduce_scatter x6, waiting for transfers between devices, step(): lax.psum_scatter(g, 'dp', scatter_dimension=0, tiled=True)  189 us
    all_gather x6, waiting for transfers between devices, step(): gather = lambda w: lax.all_gather(w, 'dp', axis=0, tiled=True)  130 us
    unnamed x27, local copies, waits for them, and re-layouts  23 us
  transfers between devices with their start and end apart: 12, of which 9 were waited for; matrix products, arithmetic and copies ran while one was open for 44% of the time, Pallas kernels for 0%

profile of v1, /device:TPU:0, one launch (start us, length us, event | category | flops | bytes accessed | tf_op | source)
XLA Modules:
  0.0 719.8 jit_solution(3913640243002899923)
XLA Ops:
  15.1 6.4 copy.10
  21.5 3.1 fusion.15
  25.2 26.9 %all-gather.13.cloned.1.call-done = bf16[1,1024,2560]{2,1,0:T(8,128)(2,1)} async-done(((bf16[1,64,2560]{2,1,0:T(8,128)(2,1)}), bf16[1,1024,2560]{2,1,0:T(8,128)(2,1)}) %all-gather.13.cloned.1.call-update) | async-done | bytes 5242896 | tf_op jit(solution)/shard_map/all_gather | solution.py:25
  52.0 18.4 %fusion.40 = f32[2048,2560]{1,0:T(8,128)} fusion(bf16[1,1024,2560]{2,1,0:T(8,128)(2,1)} %all-gather.13.cloned.1.call-done, bf16[1,2048,1024]{1,2,0:T(8,128)(2,1)} %copy.10, f32[2048]{0:T(1024)S(1)} %add_rsqrt_fusion.1), kind=kOutput, calls=%fused_computation.69 | convolution fusion | flops 10743709696 | bytes 30416896 | tf_op jit(solution)/shard_map/dot_general | solution.py:10
  70.4 22.3 %all-gather.15.cloned.1.call-done = bf16[1,1024,2560]{2,1,0:T(8,128)(2,1)} async-done(((bf16[1,64,2560]{2,1,0:T(8,128)(2,1)}), bf16[1,1024,2560]{2,1,0:T(8,128)(2,1)}) %all-gather.15.cloned.1.call-update) | async-done | bytes 5242896 | tf_op jit(solution)/shard_map/all_gather | solution.py:25
  92.7 28.7 %multiply_convert_fusion.1 = (bf16[2048,2560]{1,0:T(8,128)(2,1)}, f32[2048,2560]{1,0:T(8,128)}) fusion(f32[2048,2560]{1,0:T(8,128)} %fusion.40, bf16[1,1024,2560]{2,1,0:T(8,128)(2,1)} %all-gather.15.cloned.1.call-done, bf16[1,2048,1024]{1,2,0:T(8,128)(2,1)} %copy.10, f32[2048]{0:T(1024)S(1)} %add_rsqrt_fusion.1), kind=kOutput, calls=%fused_computation.16 | convolution fusion | flops 10775166976 | bytes 61874176 | tf_op jit(solution)/shard_map/dot_general | solution.py:10
  121.4 11.9 %all-gather.17.cloned.1.call-done = bf16[1,2560,1024]{2,1,0:T(8,128)(2,1)} async-done(((bf16[1,160,1024]{2,1,0:T(8,128)(2,1)}), bf16[1,2560,1024]{2,1,0:T(8,128)(2,1)}) %all-gather.17.cloned.1.call-update) | async-done | bytes 5242896 | tf_op jit(solution)/shard_map/all_gather | solution.py:25
  133.3 17.9 %fusion.18 = (f32[2048]{0:T(1024)S(1)}, bf16[2048,1024]{0,1:T(8,128)(2,1)}) fusion(bf16[2048,2560]{1,0:T(8,128)(2,1)} %get-tuple-element.18, bf16[1,2560,1024]{2,1,0:T(8,128)(2,1)} %all-gather.17.cloned.1.call-done, bf16[1,2048,1024]{1,2,0:T(8,128)(2,1)} %copy.10), kind=kOutput, calls=%fused_computation.38 | convolution fusion | flops 10747901952 | bytes 24125440 | tf_op jit(solution)/shard_map/dot_general | solution.py:10
  151.8 22.0 %all-gather.19.cloned.1.call-done = bf16[1,2560,1024]{2,1,0:T(8,128)(2,1)} async-done(((bf16[1,160,1024]{2,1,0:T(8,128)(2,1)}), bf16[1,2560,1024]{2,1,0:T(8,128)(2,1)}) %all-gather.19.cloned.1.call-update) | async-done | bytes 5242896 | tf_op jit(solution)/shard_map/all_gather | solution.py:25
  173.8 17.0 %convolution_convert_fusion.1 = bf16[2048,2560]{1,0:T(8,128)(2,1)} fusion(bf16[1,2560,1024]{2,1,0:T(8,128)(2,1)} %all-gather.19.cloned.1.call-done, bf16[1,2048,1024]{2,1,0:T(8,128)(2,1)} %param.6), kind=kOutput, calls=%fused_computation.27 | convolution fusion | flops 10742661120 | bytes 19922944 | tf_op jit(solution)/shard_map/dot_general | solution.py:10
  190.8 24.1 %all-gather.21.cloned.1.call-done = bf16[1,1024,2560]{2,1,0:T(8,128)(2,1)} async-done(((bf16[1,64,2560]{2,1,0:T(8,128)(2,1)}), bf16[1,1024,2560]{2,1,0:T(8,128)(2,1)}) %all-gather.21.cloned.1.call-update) | async-done | bytes 5242896 | tf_op jit(solution)/shard_map/all_gather | solution.py:25
  214.9 18.3 %fusion.28 = f32[2048,2560]{1,0:T(8,128)} fusion(bf16[1,1024,2560]{2,1,0:T(8,128)(2,1)} %all-gather.21.cloned.1.call-done, bf16[2048,1024]{0,1:T(8,128)(2,1)} %get-tuple-element.21, f32[2048]{0:T(1024)S(1)} %add_rsqrt_fusion), kind=kOutput, calls=%fused_computation.57 | convolution fusion | flops 10743709696 | bytes 30416896 | tf_op jit(solution)/shard_map/dot_general | solution.py:10
  233.2 22.8 %all-gather.23.cloned.1.call-done = bf16[1,1024,2560]{2,1,0:T(8,128)(2,1)} async-done(((bf16[1,64,2560]{2,1,0:T(8,128)(2,1)}), bf16[1,1024,2560]{2,1,0:T(8,128)(2,1)}) %all-gather.23.cloned.1.call-update) | async-done | bytes 5242896 | tf_op jit(solution)/shard_map/all_gather | solution.py:25
  256.0 34.6 %fusion.4 = (bf16[2048,2560]{1,0:T(8,128)(2,1)}, bf16[2048,2560]{1,0:T(8,128)(2,1)}, f32[2048,2560]{1,0:T(8,128)}) fusion(bf16[2048,2560]{1,0:T(8,128)(2,1)} %convolution_convert_fusion.1, f32[2048,2560]{1,0:T(8,128)} %fusion.28, bf16[1,1024,2560]{2,1,0:T(8,128)(2,1)} %all-gather.23.cloned.1.call-done, bf16[2048,1024]{0,1:T(8,128)(2,1)} %get-tuple-element.21, ...), kind=kOutput, calls=%fused_computation.8 | convolution fusion | flops 10817110016 | bytes 82845696 | tf_op jit(solution)/shard_map/dot_general | solution.py:10
  290.5 21.9 %fusion.21 = bf16[2560,1024]{1,0:T(8,128)(2,1)} fusion(f32[2048,2560]{1,0:T(8,128)} %fusion.28, f32[2048,2560]{1,0:T(8,128)} %get-tuple-element.22, bf16[1,2048,1024]{2,1,0:T(8,128)(2,1)} %param.6), kind=kOutput, calls=%fused_computation.45 | convolution fusion | flops 10771496960 | bytes 51380224 | tf_op jit(solution)/shard_map/dot_general | solution.py:10
  312.6 7.0 copy.9
  319.5 17.4 %fusion.22 = f32[2048,1024]{0,1:T(8,128)} fusion(bf16[2048,2560]{1,0:T(8,128)(2,1)} %get-tuple-element.11, bf16[1,1024,2560]{2,1,0:T(8,128)(2,1)} %all-gather.23.cloned.1.call-done), kind=kOutput, calls=%fused_computation.51 | convolution fusion | flops 10737418240 | bytes 24117248 | tf_op jit(solution)/shard_map/dot_general | solution.py:10
  336.9 16.9 %fusion.20 = (f32[2048]{0:T(1024)S(1)}, bf16[2048,1024]{0,1:T(8,128)(2,1)S(1)}) fusion(bf16[2048,1024]{0,1:T(8,128)(2,1)S(1)} %copy-done.5, f32[2048,1024]{0,1:T(8,128)} %fusion.22, bf16[2048,2560]{1,0:T(8,128)(2,1)} %get-tuple-element.10, bf16[1,1024,2560]{2,1,0:T(8,128)(2,1)} %all-gather.21.cloned.1.call-done), kind=kOutput, calls=%fused_computation.40 | convolution fusion | flops 10749999104 | bytes 32514048 | tf_op jit(solution)/shard_map/dot_general | solution.py:10
  353.9 3.3 add_convert_fusion.2
  359.2 15.6 %convolution_convert_fusion.2 = bf16[2560,1024]{1,0:T(8,128)(2,1)} fusion(bf16[2048,2560]{1,0:T(8,128)(2,1)} %get-tuple-element.18, bf16[2048,1024]{0,1:T(8,128)(2,1)S(1)} %add_convert_fusion.2), kind=kOutput, calls=%fused_computation.46 | convolution fusion | flops 10740039680 | bytes 19922944 | tf_op jit(solution)/shard_map/dot_general | solution.py:10
  374.8 16.6 %convolution_convert_fusion.3 = bf16[1024,2560]{1,0:T(8,128)(2,1)} fusion(bf16[2048,2560]{1,0:T(8,128)(2,1)} %get-tuple-element.10, bf16[2048,1024]{0,1:T(8,128)(2,1)} %get-tuple-element.21, f32[2048]{0:T(1024)S(1)} %add_rsqrt_fusion), kind=kOutput, calls=%fused_computation.47 | convolution fusion | flops 10746331136 | bytes 19931136 | tf_op jit(solution)/shard_map/dot_general | solution.py:10
  391.5 31.9 %fusion.7 = (bf16[2048,2560]{1,0:T(8,128)(2,1)}, bf16[2048,2560]{1,0:T(8,128)(2,1)}) fusion(f32[2048,2560]{1,0:T(8,128)} %get-tuple-element.19, f32[2048,2560]{1,0:T(8,128)} %fusion.40, bf16[2048,1024]{0,1:T(8,128)(2,1)} %copy-done.2, bf16[1,2560,1024]{2,1,0:T(8,128)(2,1)} %all-gather.17.cloned.1.call-done), kind=kOutput, calls=%fused_computation.11 | convolution fusion | flops 10816061440 | bytes 72351744 | tf_op jit(solution)/shard_map/dot_general | solution.py:10
  423.4 15.3 %convolution_convert_fusion.4 = bf16[1024,2560]{1,0:T(8,128)(2,1)} fusion(bf16[2048,2560]{1,0:T(8,128)(2,1)} %get-tuple-element.9, bf16[1,2048,1024]{1,2,0:T(8,128)(2,1)S(1)} %copy-done, f32[2048]{0:T(1024)S(1)} %copy-done.9), kind=kOutput, calls=%fused_computation.48 | convolution fusion | flops 10746331136 | bytes 19931136 | tf_op jit(solution)/shard_map/dot_general | solution.py:10
  438.8 16.6 %convolution_convert_fusion.5 = bf16[1024,2560]{1,0:T(8,128)(2,1)} fusion(bf16[2048,2560]{1,0:T(8,128)(2,1)} %get-tuple-element.11, bf16[2048,1024]{0,1:T(8,128)(2,1)} %get-tuple-element.21, f32[2048]{0:T(1024)S(1)} %add_rsqrt_fusion), kind=kOutput, calls=%fused_computation.49 | convolution fusion | flops 10746331136 | bytes 19931136 | tf_op jit(solution)/shard_map/dot_general | solution.py:10
  455.4 16.7 %convolution_convert_fusion.6 = bf16[1024,2560]{1,0:T(8,128)(2,1)} fusion(bf16[2048,2560]{1,0:T(8,128)(2,1)} %get-tuple-element.8, bf16[1,2048,1024]{1,2,0:T(8,128)(2,1)} %copy.10, f32[2048]{0:T(1024)S(1)} %copy-done.9), kind=kOutput, calls=%fused_computation.50 | convolution fusion | flops 10746331136 | bytes 19931136 | tf_op jit(solution)/shard_map/dot_general | solution.py:10
  472.2 17.4 %fusion.34 = f32[2048,1024]{0,1:T(8,128)} fusion(bf16[2048,2560]{1,0:T(8,128)(2,1)} %get-tuple-element.9, bf16[1,1024,2560]{2,1,0:T(8,128)(2,1)} %all-gather.15.cloned.1.call-done), kind=kOutput, calls=%fused_computation.63 | convolution fusion | flops 10737418240 | bytes 24117248 | tf_op jit(solution)/shard_map/dot_general | solution.py:10
  489.6 16.9 %fusion.17 = (f32[2048]{0:T(1024)S(1)}, bf16[2048,1024]{0,1:T(8,128)(2,1)S(1)}) fusion(bf16[1,2048,1024]{1,2,0:T(8,128)(2,1)S(1)} %copy-done.1, f32[2048,1024]{0,1:T(8,128)} %fusion.34, bf16[2048,2560]{1,0:T(8,128)(2,1)} %get-tuple-element.8, bf16[1,1024,2560]{2,1,0:T(8,128)(2,1)} %all-gather.13.cloned.1.call-done), kind=kOutput, calls=%fused_computation.37 | convolution fusion | flops 10749999104 | bytes 32514048 | tf_op jit(solution)/shard_map/dot_general | solution.py:10
  506.6 4.7 fusion.42
  511.3 6.4 copy.11
  519.6 57.0 %reduce-scatter.11.cloned.1.call-done = bf16[64,2560]{1,0:T(8,128)(2,1)} async-done(((bf16[1024,2560]{1,0:T(8,128)(2,1)}), bf16[64,2560]{1,0:T(8,128)(2,1)}) %reduce-scatter.11.cloned.1.call-update) | async-done | bytes 327696 | tf_op jit(solution)/shard_map/reduce_scatter | solution.py:26
  578.6 66.1 %reduce-scatter.9.cloned.1.call-done = bf16[64,2560]{1,0:T(8,128)(2,1)} async-done(((bf16[1024,2560]{1,0:T(8,128)(2,1)}), bf16[64,2560]{1,0:T(8,128)(2,1)}) %reduce-scatter.9.cloned.1.call-update) | async-done | bytes 327696 | tf_op jit(solution)/shard_map/reduce_scatter | solution.py:26
  644.7 65.9 %reduce-scatter.7.cloned.1.call-done = bf16[64,2560]{1,0:T(8,128)(2,1)} async-done(((bf16[1024,2560]{1,0:T(8,128)(2,1)}), bf16[64,2560]{1,0:T(8,128)(2,1)}) %reduce-scatter.7.cloned.1.call-update) | async-done | bytes 327696 | tf_op jit(solution)/shard_map/reduce_scatter | solution.py:26
  (61 shorter events, 17.3 us)
Async XLA Ops:
  7.2 44.9 %all-gather.13.cloned.1.call-start = ((), (), s32[]{:S(2)}) async-start(), calls=%async_computation.12 | async-start | bytes 5570560 | tf_op jit(solution)/shard_map/all_gather | solution.py:25
  9.2 83.5 %all-gather.15.cloned.1.call-start = ((), (), s32[]{:S(2)}) async-start(), calls=%async_computation.13 | async-start | bytes 5570560 | tf_op jit(solution)/shard_map/all_gather | solution.py:25
  11.2 122.1 %all-gather.17.cloned.1.call-start = ((), (), s32[]{:S(2)}) async-start(), calls=%async_computation.14 | async-start | bytes 5570560 | tf_op jit(solution)/shard_map/all_gather | solution.py:25
  13.3 160.6 %all-gather.19.cloned.1.call-start = ((), (), s32[]{:S(2)}) async-start(), calls=%async_computation.15 | async-start | bytes 5570560 | tf_op jit(solution)/shard_map/all_gather | solution.py:25
  13.8 201.0 %all-gather.21.cloned.1.call-start = ((), (), s32[]{:S(2)}) async-start(), calls=%async_computation.16 | async-start | bytes 5570560 | tf_op jit(solution)/shard_map/all_gather | solution.py:25
  14.4 241.5 %all-gather.23.cloned.1.call-start = ((), (), s32[]{:S(2)}) async-start(), calls=%async_computation.17 | async-start | bytes 5570560 | tf_op jit(solution)/shard_map/all_gather | solution.py:25
  15.0 502.7 %reduce-scatter.17.cloned.1.call-start = ((), (), s32[]{:S(2)}) async-start(), calls=%async_computation.11 | async-start | bytes 5570560 | tf_op jit(solution)/shard_map/reduce_scatter | solution.py:26
  24.6 0.6 copy-start.6
  25.2 67.5 %copy-start.8 = (f32[2048]{0:T(1024)}, f32[2048]{0:T(1024)S(1)}, u32[]{:S(2)}) copy-start(f32[2048]{0:T(1024)S(1)} %add_rsqrt_fusion.1) | copy-start | bytes 24580
  151.2 0.6 copy-start.10
  312.5 205.2 %reduce-scatter.15.cloned.1.call-start = ((), (), s32[]{:S(2)}) async-start(), calls=%async_computation.10 | async-start | bytes 5570560 | tf_op jit(solution)/shard_map/reduce_scatter | solution.py:26
  319.5 17.4 %copy-start.5 = (bf16[2048,1024]{0,1:T(8,128)(2,1)S(1)}, bf16[2048,1024]{0,1:T(8,128)(2,1)}, u32[]{:S(2)}) copy-start(bf16[2048,1024]{0,1:T(8,128)(2,1)} %get-tuple-element.21) | copy-start | bytes 12582916
  336.9 16.9 %copy-start.11 = (f32[2048]{0:T(1024)S(1)}, f32[2048]{0:T(1024)}, u32[]{:S(2)}) copy-start(f32[2048]{0:T(1024)} %copy-done.10) | copy-start | bytes 24580
  336.9 16.9 %copy-start.4 = (bf16[1,2048,1024]{1,2,0:T(8,128)(2,1)S(1)}, bf16[1,2048,1024]{1,2,0:T(8,128)(2,1)}, u32[]{:S(2)}) copy-start(bf16[1,2048,1024]{1,2,0:T(8,128)(2,1)} %copy.9) | copy-start | bytes 12582916
  357.2 2.0 copy-start.2
  374.8 144.9 %reduce-scatter.13.cloned.1.call-start = ((), (), s32[]{:S(2)}) async-start(), calls=%async_computation.9 | async-start | bytes 5570560 | tf_op jit(solution)/shard_map/reduce_scatter | solution.py:26
  391.5 185.1 %reduce-scatter.11.cloned.1.call-start = ((), (), s32[]{:S(2)}) async-start(), calls=%async_computation.8 | async-start | bytes 5570560 | tf_op jit(solution)/shard_map/reduce_scatter | solution.py:26
  391.5 31.9 %copy-start = (bf16[1,2048,1024]{1,2,0:T(8,128)(2,1)S(1)}, bf16[1,2048,1024]{1,2,0:T(8,128)(2,1)}, u32[]{:S(2)}) copy-start(bf16[1,2048,1024]{1,2,0:T(8,128)(2,1)} %copy.10) | copy-start | bytes 12582916
  391.5 31.9 %copy-start.9 = (f32[2048]{0:T(1024)S(1)}, f32[2048]{0:T(1024)}, u32[]{:S(2)}) copy-start(f32[2048]{0:T(1024)} %copy-done.8) | copy-start | bytes 24580
  438.7 205.9 %reduce-scatter.9.cloned.1.call-start = ((), (), s32[]{:S(2)}) async-start(), calls=%async_computation.7 | async-start | bytes 5570560 | tf_op jit(solution)/shard_map/reduce_scatter | solution.py:26
  455.4 255.2 %reduce-scatter.7.cloned.1.call-start = ((), (), s32[]{:S(2)}) async-start(), calls=%async_computation.6 | async-start | bytes 5570560 | tf_op jit(solution)/shard_map/reduce_scatter | solution.py:26
  472.2 17.4 %copy-start.1 = (bf16[1,2048,1024]{1,2,0:T(8,128)(2,1)S(1)}, bf16[1,2048,1024]{1,2,0:T(8,128)(2,1)}, u32[]{:S(2)}) copy-start(bf16[1,2048,1024]{1,2,0:T(8,128)(2,1)} %copy.10) | copy-start | bytes 12582916
  489.6 16.9 %copy-start.7 = (f32[2048]{0:T(1024)S(1)}, f32[2048]{0:T(1024)}, u32[]{:S(2)}) copy-start(f32[2048]{0:T(1024)} %copy-done.6) | copy-start | bytes 24580
  489.6 17.0 %copy-start.3 = (bf16[2048,1024]{0,1:T(8,128)(2,1)S(1)}, bf16[2048,1024]{0,1:T(8,128)(2,1)}, u32[]{:S(2)}) copy-start(bf16[2048,1024]{0,1:T(8,128)(2,1)} %copy-done.2) | copy-start | bytes 12582916
Sparse Core Ops, SparseCore 0:
  10.8 41.1 all-gather.12
  54.3 38.3 all-gather.14
  94.9 38.3 all-gather.16
  135.4 38.3 all-gather.18
  176.5 38.3 all-gather.20
  217.5 38.3 all-gather.22
  312.6 63.4 reduce-scatter.16
  378.4 64.4 reduce-scatter.14
  445.2 64.6 reduce-scatter.12
  512.0 64.5 reduce-scatter.10
  578.9 65.7 reduce-scatter.8
  646.8 63.7 reduce-scatter.6
